TPU v7x, 32 devices: a whole 2x2x4 slice. The times are simulated.
32 devices in a mesh: gx: 16 (over z, y, x), gz: 2 (over core).
Axes of the slice: x: 2, y: 2, z: 4, core: 2. Of those that a mesh axis runs over, the one named last changes fastest.
Arguments:
- state: float32 [5, 128, 16, 256], P(None, 'gx', None, 'gz'), may hold values from -1 to 8.5, as said below
- register: float32 [5, 128, 16, 256], P(None, 'gx', None, 'gz'), may hold values from -2.4 to 2.4
- top_ghost: float32 [5, 128, 3, 256], P(None, 'gx', None, 'gz'), may hold values from -1 to 8.5, as said below
- flags: int32 [128, 16, 2], P('gx', None, 'gz'), may hold values 0 or 1
Outputs:
- new_state: float32 [5, 128, 16, 256], P(None, 'gx', None, 'gz')
- new_register: float32 [5, 128, 16, 256], P(None, 'gx', None, 'gz')
Inputs may be any that keep to these rules, and one draw needn't show every extreme that they name: `state`: conserved variables of an ideal gas with ratio of heats 1.4, density 0.5 to 2 and pressure 0.3 to 1.5 in every cell. `top_ghost`: conserved variables of an ideal gas with ratio of heats 1.4, density 0.5 to 2 and pressure 0.3 to 1.5 in every cell.
All inputs are finite; a program needn't handle non-finite values. No bound on the sum of `flags` on one device may be relied on, other than what follows from the above.
Results may differ from a plain program's by a relative error of at most 0.0003.
Values sent between devices are 32-bit elements; how exact they have to be, the bound alone decides.
A program may use at most 64 MiB of HBM per device.

v0:
```python
import jax
import jax.numpy as jnp
from jax import lax
from jax.sharding import PartitionSpec as P

ZBLOCK = 128


GAMMA = 1.4
EPS_WENO = 1e-06
LAMBDA_X = 0.1
LAMBDA_Y = 0.15
LAMBDA_Z = 0.1
REGISTER_DECAY = -5.0 / 9.0
UPDATE_WEIGHT = 15.0 / 16.0


def extended(block, sides, width):
    for axis, dim in sides:
        count = lax.axis_size(axis)
        forward = [(i, i + 1) for i in range(count - 1)]
        forward.append((count - 1, 0))
        backward = [(target, source) for source, target in forward]
        low = lax.ppermute(
            lax.slice_in_dim(block, block.shape[dim] - width, None, axis=dim), axis, forward
        )
        high = lax.ppermute(lax.slice_in_dim(block, 0, width, axis=dim), axis, backward)
        block = jnp.concatenate([low, block, high], axis=dim)
    return block


def primitives(cons):
    density = cons[0]
    inverse = 1.0 / density
    vel_x = cons[1] * inverse
    vel_y = cons[2] * inverse
    vel_z = cons[3] * inverse
    pressure = (GAMMA - 1.0) * (
        cons[4] - 0.5 * (cons[1] * vel_x + cons[2] * vel_y + cons[3] * vel_z)
    )
    return (density, vel_x, vel_y, vel_z, pressure)


def global_speeds(prims):
    density, vel_x, vel_y, vel_z, pressure = prims
    sound = jnp.sqrt(GAMMA * pressure / density)
    local = jnp.stack(
        [
            jnp.max(jnp.abs(vel_x) + sound),
            jnp.max(jnp.abs(vel_y) + sound),
            jnp.max(jnp.abs(vel_z) + sound),
        ]
    )
    return lax.pmax(local, ("gx", "gz"))


def physical_flux(cons, prims, var):
    pressure = prims[4]
    velocity = prims[var]
    rows = [
        cons[0] * velocity,
        cons[1] * velocity,
        cons[2] * velocity,
        cons[3] * velocity,
        (cons[4] + pressure) * velocity,
    ]
    rows[var] = rows[var] + pressure
    return jnp.stack(rows)


def weno_face(vals):
    first, second, third, fourth, fifth = vals
    cand_a = (2.0 * first - 7.0 * second + 11.0 * third) / 6.0
    cand_b = (-second + 5.0 * third + 2.0 * fourth) / 6.0
    cand_c = (2.0 * third + 5.0 * fourth - fifth) / 6.0
    smooth_a = (
        13.0 / 12.0 * (first - 2.0 * second + third) ** 2
        + 0.25 * (first - 4.0 * second + 3.0 * third) ** 2
    )
    smooth_b = 13.0 / 12.0 * (second - 2.0 * third + fourth) ** 2 + 0.25 * (second - fourth) ** 2
    smooth_c = (
        13.0 / 12.0 * (third - 2.0 * fourth + fifth) ** 2
        + 0.25 * (3.0 * third - 4.0 * fourth + fifth) ** 2
    )
    weight_a = 0.1 / (EPS_WENO + smooth_a) ** 2
    weight_b = 0.6 / (EPS_WENO + smooth_b) ** 2
    weight_c = 0.3 / (EPS_WENO + smooth_c) ** 2
    return (weight_a * cand_a + weight_b * cand_b + weight_c * cand_c) / (
        weight_a + weight_b + weight_c
    )


def divergence(padded, prims, alpha, var, axis_pos, count, cell_flag):
    flux = physical_flux(padded, prims, var)
    plus = 0.5 * (flux + alpha * padded)
    minus = 0.5 * (flux - alpha * padded)

    def window(arr, offset):
        return lax.slice_in_dim(arr, offset, offset + count + 1, axis=axis_pos)

    central = (
        37.0 * (window(flux, 2) + window(flux, 3))
        - 8.0 * (window(flux, 1) + window(flux, 4))
        + (window(flux, 0) + window(flux, 5))
    ) / 60.0
    upwind = weno_face(
        [window(plus, 0), window(plus, 1), window(plus, 2), window(plus, 3), window(plus, 4)]
    )
    upwind = upwind + weno_face(
        [window(minus, 5), window(minus, 4), window(minus, 3), window(minus, 2), window(minus, 1)]
    )

    def jump(face):
        return lax.slice_in_dim(face, 1, count + 1, axis=axis_pos) - lax.slice_in_dim(
            face, 0, count, axis=axis_pos
        )

    return jnp.where(cell_flag[None], jump(upwind), jump(central))


def wall_pad(inner, top_ghost):
    mirror = jnp.array([1.0, 1.0, -1.0, 1.0, 1.0], dtype=jnp.float32).reshape(5, 1, 1, 1)
    lower = jnp.flip(inner[:, :, :3], axis=2) * mirror
    return jnp.concatenate([lower, inner, top_ghost], axis=2)


def expand_flags(flags):
    shape = flags.shape
    wide = jnp.broadcast_to(flags[:, :, :, None], (shape[0], shape[1], shape[2], ZBLOCK))
    return wide.reshape(shape[0], shape[1], shape[2] * ZBLOCK) > 0


def shards(state, register, top_ghost, flags):
    cell_flag = expand_flags(flags)
    x_pad = extended(state, (("gx", 1),), 3)
    z_pad = extended(state, (("gz", 3),), 3)
    y_pad = wall_pad(state, top_ghost)
    x_prims = primitives(x_pad)
    alpha = global_speeds(primitives(state))
    div_x = divergence(x_pad, x_prims, alpha[0], 1, 1, state.shape[1], cell_flag)
    div_y = divergence(y_pad, primitives(y_pad), alpha[1], 2, 2, state.shape[2], cell_flag)
    div_z = divergence(z_pad, primitives(z_pad), alpha[2], 3, 3, state.shape[3], cell_flag)
    change = -(LAMBDA_X * div_x + LAMBDA_Y * div_y + LAMBDA_Z * div_z)
    new_register = REGISTER_DECAY * register + change
    new_state = state + UPDATE_WEIGHT * new_register
    return (new_state, new_register)


def solution(mesh):
    return jax.shard_map(
        shards,
        mesh=mesh,
        in_specs=(
            P(None, "gx", None, "gz"),
            P(None, "gx", None, "gz"),
            P(None, "gx", None, "gz"),
            P("gx", None, "gz"),
        ),
        out_specs=(P(None, "gx", None, "gz"), P(None, "gx", None, "gz")),
        check_vma=False,
    )
```

profile of v0, /device:TPU:0, one launch (start us, length us, event | category | flops | bytes accessed | tf_op | source)
XLA Modules:
  0.0 66.9 jit_solution(10679124771426530902)
XLA Ops:
  0.6 1.1 %copy.20 = f32[5,8,16,128]{3,1,2,0:T(8,128)S(1)} copy(f32[5,8,16,128]{3,2,1,0:T(8,128)} %param.5) | data formatting | bytes 655360 | tf_op args[0]
  1.8 3.0 %collective-permute-start = (f32[5,3,16,128]{3,1,2,0:T(4,128)S(1)}, f32[5,3,16,128]{3,1,2,0:T(4,128)S(1)}, u32[]{:S(2)}, u32[]{:S(2)}) collective-permute-start(f32[5,3,16,128]{3,1,2,0:T(4,128)S(1)} %get-tuple-element.27), channel_id=1, source_target_pairs={{0,2},{2,4},{4,6},{6,8},{8,10},{10,12},{12,14},{14,16},{16,18},{18... | collective-permute-start | bytes 368648 | tf_op jit(solution)/shard_map/ppermute | solution.py:24
  4.8 4.1 %collective-permute-start.1 = (f32[5,3,16,128]{3,1,2,0:T(4,128)S(1)}, f32[5,3,16,128]{3,1,2,0:T(4,128)S(1)}, u32[]{:S(2)}, u32[]{:S(2)}) collective-permute-start(f32[5,3,16,128]{3,1,2,0:T(4,128)S(1)} %get-tuple-element.28), channel_id=1, source_target_pairs={{2,0},{4,2},{6,4},{8,6},{10,8},{12,10},{14,12},{16,14},{18,16},{20... | collective-permute-start | bytes 368648 | tf_op jit(solution)/shard_map/ppermute | solution.py:27
  8.9 0.2 fusion.52
  9.1 0.5 collective-permute-start.3
  9.6 0.7 %add_reduce_fusion.2 = (f32[]{:T(128)}, f32[]{:T(128)}, f32[]{:T(128)}) fusion(f32[5,8,16,128]{3,2,1,0:T(8,128)S(1)} %copy-done), kind=kLoop, calls=%fused_computation.115 | loop fusion | flops 360445 | bytes 327692 | tf_op jit(solution)/shard_map/reduce_max | solution.py:49
  10.3 2.0 %pad_maximum_fusion.3 = f32[3]{0:T(128)S(1)} fusion(f32[1]{0:T(128)} %bitcast.9, f32[1]{0:T(128)} %bitcast.8, f32[1]{0:T(128)} %bitcast.7), kind=kLoop, calls=%fused_computation.118 | loop fusion | flops 6 | bytes 24 | tf_op jit(solution)/shard_map/stack | solution.py:47
  12.3 37.7 %pmax.7 = f32[3]{0:T(128)S(1)} all-reduce(f32[3]{0:T(128)S(1)} %pad_maximum_fusion.3), channel_id=1, replica_groups=mesh['gx'=16,'gz'=2] {'gx','gz'}, use_global_device_ids=true, to_apply=%region_3.4 | all-reduce | flops 3 | bytes 24 | tf_op jit(solution)/shard_map/pmax | solution.py:54
  50.0 0.6 fusion.53
  50.7 0.8 %copy-done.2 = f32[5,8,3,128]{3,1,2,0:T(8,128)S(1)} copy-done((f32[5,8,3,128]{3,1,2,0:T(8,128)S(1)}, f32[5,8,3,128]{3,1,2,0:T(8,128)}, u32[]{:S(2)}) %copy-start.2) | copy-done | bytes 61464
  51.7 0.7 %add_multiply_fusion.2 = (f32[5,8,22,128]{3,1,2,0:T(8,128)S(1)}, f32[5,8,22,128]{3,1,2,0:T(8,128)S(1)}) fusion(f32[5,8,22,128]{3,1,2,0:T(8,128)S(1)} %multiply_dynamic-update-slice_fusion.8, f32[]{:T(128)} %bitcast.11, f32[5,8,3,128]{3,1,2,0:T(8,128)S(1)} %copy-done.2, f32[5,8,16,128]{3,1,2,0:T(8,128)S(1)} %copy.20, f32[5,8,3,128]{3,1,2,0:T(8,128)S(1)} %reverse_multiply_fusion), kind=kLoop, calls=%fused_computation.26 | loop fusion | flops 788480 | bytes 1802244 | tf_op jit(solution)/shard_map/mul | solution.py:95
  52.4 1.6 %fusion.11 = (f32[5,8,17,128]{3,1,2,0:T(8,128)S(1)}, f32[5,8,17,128]{3,1,2,0:T(8,128)S(1)}) fusion(f32[5,8,22,128]{3,1,2,0:T(8,128)S(1)} %multiply_dynamic-update-slice_fusion.8, f32[5,8,22,128]{3,1,2,0:T(8,128)S(1)} %get-tuple-element.26, f32[5,8,22,128]{3,1,2,0:T(8,128)S(1)} %get-tuple-element.25), kind=kLoop, calls=%fused_computation.29 | loop fusion | flops 11924480 | bytes 6266880 | tf_op jit(solution)/shard_map/div | solution.py:101
  54.1 0.1 copy.11
  54.2 0.3 pad_maximum_fusion.1
  54.7 0.8 %add_multiply_fusion = (f32[5,8,16,134]{3,1,2,0:T(8,128)S(1)}, f32[5,8,16,134]{3,1,2,0:T(8,128)S(1)}) fusion(f32[5,8,16,134]{3,1,2,0:T(8,128)S(1)} %multiply_dynamic-update-slice_fusion, f32[5,8,16,134]{3,1,2,0:T(8,128)S(1)} %pad_maximum_fusion.1, f32[]{:T(128)} %bitcast.12), kind=kLoop, calls=%fused_computation.20 | loop fusion | flops 428800 | bytes 1372164 | tf_op jit(solution)/shard_map/mul | solution.py:95
  55.5 3.3 %divide_add_fusion = f32[5,8,16,129]{3,1,2,0:T(8,128)S(1)} fusion(f32[5,8,16,134]{3,1,2,0:T(8,128)S(1)} %get-tuple-element.24, f32[5,8,16,134]{3,1,2,0:T(8,128)S(1)} %get-tuple-element.23), kind=kLoop, calls=%fused_computation.18 | loop fusion | flops 10650240 | bytes 3632640 | tf_op jit(solution)/shard_map/add | solution.py:109
  58.8 0.9 %fusion.1 = f32[5,8,16,129]{3,1,2,0:T(8,128)S(1)} fusion(f32[5,8,16,134]{3,1,2,0:T(8,128)S(1)} %multiply_dynamic-update-slice_fusion), kind=kLoop, calls=%fused_computation.2 | loop fusion | flops 660480 | bytes 2311680 | tf_op jit(solution)/shard_map/div | solution.py:101
  59.7 0.1 pad_maximum_fusion
  60.0 0.4 fusion.6
  60.4 0.9 %add_multiply_fusion.1 = (f32[5,14,16,128]{3,1,2,0:T(8,128)S(1)}, f32[5,14,16,128]{3,1,2,0:T(8,128)S(1)}) fusion(f32[5,14,16,128]{3,1,2,0:T(8,128)S(1)} %multiply_dynamic-update-slice_fusion.4, f32[]{:T(128)} %bitcast.10, f32[5,3,16,128]{3,1,2,0:T(4,128)S(1)} %collective-permute-done.1, f32[5,8,16,128]{3,1,2,0:T(8,128)S(1)} %copy.20, ...), kind=kLoop, calls=%fused_computation.23 | loop fusion | flops 1003520 | bytes 2293764 | tf_op jit(solution)/shard_map/mul | solution.py:95
  61.3 3.3 %divide_add_fusion.1 = f32[5,9,16,128]{3,1,2,0:T(8,128)S(1)} fusion(f32[5,14,16,128]{3,1,2,0:T(8,128)S(1)} %get-tuple-element.22, f32[5,14,16,128]{3,1,2,0:T(8,128)S(1)} %get-tuple-element.21), kind=kLoop, calls=%fused_computation.21 | loop fusion | flops 11888640 | bytes 4055040 | tf_op jit(solution)/shard_map/add | solution.py:109
  64.7 0.6 multiply_add_fusion
  65.3 0.8 %copy.21 = f32[5,8,16,128]{3,2,1,0:T(8,128)} copy(f32[5,8,16,128]{3,1,2,0:T(8,128)S(1)} %get-tuple-element.7) | data formatting | bytes 655360
  66.1 0.8 %copy.22 = f32[5,8,16,128]{3,2,1,0:T(8,128)} copy(f32[5,8,16,128]{3,1,2,0:T(8,128)S(1)} %get-tuple-element.8) | data formatting | bytes 655360
  (34 shorter events, 0.7 us)
Async XLA Ops:
  1.8 57.9 %collective-permute-start = (f32[5,3,16,128]{3,1,2,0:T(4,128)S(1)}, f32[5,3,16,128]{3,1,2,0:T(4,128)S(1)}, u32[]{:S(2)}, u32[]{:S(2)}) collective-permute-start(f32[5,3,16,128]{3,1,2,0:T(4,128)S(1)} %get-tuple-element.27), channel_id=1, source_target_pairs={{0,2},{2,4},{4,6},{6,8},{8,10},{10,12},{12,14},{14,16},{16,18},{18... | collective-permute-start | bytes 368648 | tf_op jit(solution)/shard_map/ppermute | solution.py:24
  4.8 4.8 %copy-start = (f32[5,8,16,128]{3,2,1,0:T(8,128)S(1)}, f32[5,8,16,128]{3,2,1,0:T(8,128)}, u32[]{:S(2)}) copy-start(f32[5,8,16,128]{3,2,1,0:T(8,128)} %param.5) | copy-start | bytes 983044
  4.8 54.9 %collective-permute-start.1 = (f32[5,3,16,128]{3,1,2,0:T(4,128)S(1)}, f32[5,3,16,128]{3,1,2,0:T(4,128)S(1)}, u32[]{:S(2)}, u32[]{:S(2)}) collective-permute-start(f32[5,3,16,128]{3,1,2,0:T(4,128)S(1)} %get-tuple-element.28), channel_id=1, source_target_pairs={{2,0},{4,2},{6,4},{8,6},{10,8},{12,10},{14,12},{16,14},{18,16},{20... | collective-permute-start | bytes 368648 | tf_op jit(solution)/shard_map/ppermute | solution.py:27
  9.0 45.2 %collective-permute-start.2 = (f32[5,8,16,3]{3,1,2,0:T(8,128)S(1)}, f32[5,8,16,3]{3,1,2,0:T(8,128)S(1)}, u32[]{:S(2)}, u32[]{:S(2)}) collective-permute-start(f32[5,8,16,3]{3,1,2,0:T(8,128)S(1)} %get-tuple-element.29), channel_id=1, source_target_pairs={{0,1},{1,0},{2,3},{3,2},{4,5},{5,4},{6,7},{7,6},{8,9},{9,8},{10,11... | collective-permute-start | bytes 23048 | tf_op jit(solution)/shard_map/ppermute | solution.py:24
  9.1 45.1 %collective-permute-start.3 = (f32[5,8,16,3]{3,1,2,0:T(8,128)S(1)}, f32[5,8,16,3]{3,1,2,0:T(8,128)S(1)}, u32[]{:S(2)}, u32[]{:S(2)}) collective-permute-start(f32[5,8,16,3]{3,1,2,0:T(8,128)S(1)} %get-tuple-element.30), channel_id=1, source_target_pairs={{1,0},{0,1},{3,2},{2,3},{5,4},{4,5},{7,6},{6,7},{9,8},{8,9},{11,10... | collective-permute-start | bytes 23048 | tf_op jit(solution)/shard_map/ppermute | solution.py:27
  50.0 0.7 copy-start.4
  50.7 0.8 %copy-start.2 = (f32[5,8,3,128]{3,1,2,0:T(8,128)S(1)}, f32[5,8,3,128]{3,1,2,0:T(8,128)}, u32[]{:S(2)}) copy-start(f32[5,8,3,128]{3,1,2,0:T(8,128)} %param.7) | copy-start | bytes 184324
  52.4 1.7 %copy-start.3 = (s32[8,16,1]{1,2,0:T(1,128)S(1)}, s32[8,16,1]{1,2,0:T(1,128)}, u32[]{:S(2)}) copy-start(s32[8,16,1]{1,2,0:T(1,128)} %param.8) | copy-start | bytes 1540
  61.3 3.3 %copy-start.1 = (f32[5,8,16,128]{3,2,1,0:T(8,128)S(1)}, f32[5,8,16,128]{3,2,1,0:T(8,128)}, u32[]{:S(2)}) copy-start(f32[5,8,16,128]{3,2,1,0:T(8,128)} %param.6) | copy-start | bytes 983044
where the time goes:
time: 67.2 us; the launch traced here: 66.9 us
  blocking collectives  37.7 us (56%)
  other arithmetic  16.2 us (24%)
  starting transfers between devices  7.66 us (11%)
  local copies, waits for them, and re-layouts  4.38 us (7%)
  between operations  0.87 us (1%)
    pmax x1, blocking collectives, global_speeds(): return lax.pmax(local, ('gx', 'gz'))  37.7 us
    add x2, other arithmetic, divergence(): upwind + weno_face([window(minus, 5), window(minus, 4), window(minus, 3),...  6.6 us
    ppermute x2, starting transfers between devices, extended(): lax.ppermute(lax.slice_in_dim(block, 0, width, axis=dim), axis, backward)  4.57 us
    unnamed x13, local copies, waits for them, and re-layouts  3.47 us
    ppermute x2, starting transfers between devices, extended(): lax.ppermute(lax.slice_in_dim(block, block.shape[dim] - width, None, axis...  3.09 us
    div x3, other arithmetic, divergence(): (37.0 * (window(flux, 2) + window(flux, 3)) - 8.0 * (window(flux, 1) + wi...  2.93 us
    mul x3, other arithmetic, divergence(): plus = 0.5 * (flux + alpha * padded)  2.39 us
    another operation x1, other arithmetic, global_speeds(): jnp.stack([jnp.max(jnp.abs(vel_x) + sound), jnp.max(jnp.abs(vel_y) + soun...  2 us
  transfers between devices with their start and end apart: 4, of which 0 were waited for; matrix products, arithmetic and copies ran while one was open for 17% of the time, Pallas kernels for 0%

commit v1 on v0

v1 whole, which is shorter than its diff:
```python
import functools

import jax
import jax.numpy as jnp
from jax import lax
from jax.experimental import pallas as pl
from jax.experimental.pallas import tpu as pltpu
from jax.sharding import PartitionSpec as P

MESH = pl.DeviceIdType.MESH
GAMMA = 1.4
EPS_WENO = 1e-06
LAMBDA = (0.1, 0.15, 0.1)
REGISTER_DECAY = -5.0 / 9.0
UPDATE_WEIGHT = 15.0 / 16.0
UNROLL_LIMIT = 64


def reciprocal(value):
    guess = pl.reciprocal(value, approx=True)
    return guess * (2.0 - value * guess)


def pressure_velocity(cons):
    inverse = reciprocal(cons[0])
    vel = [cons[1] * inverse, cons[2] * inverse, cons[3] * inverse]
    pressure = (GAMMA - 1.0) * (
        cons[4] - 0.5 * (cons[1] * vel[0] + cons[2] * vel[1] + cons[3] * vel[2])
    )
    return inverse, vel, pressure


def shifted(me, step, count):
    moved = me + step
    return jnp.where(moved >= count, moved - count, moved)


def exchange_kernel(
    ngx, ngz, ny, state_ref, xpad, zt, alpha_ref, slots, mine, load_sem, send_sem, recv_sem,
    halo_send, halo_recv
):
    gx, gz = lax.axis_index("gx"), lax.axis_index("gz")
    rows = state_ref.shape[1]
    halo = 3 * ny
    load = pltpu.make_async_copy(state_ref, xpad.at[:, pl.ds(halo, rows), :], load_sem)
    load.start()
    barrier = pltpu.get_barrier_semaphore()
    offsets = [(dx, dz) for dx in range(ngx) for dz in range(ngz)][1:]
    peers = len(offsets)

    def each_peer(action):
        if peers < UNROLL_LIMIT:
            for slot, (dx, dz) in enumerate(offsets):
                action(slot, shifted(gx, dx, ngx), shifted(gz, dz, ngz))
        else:
            def body(slot, carry):
                dx, dz = (slot + 1) // ngz, (slot + 1) % ngz
                action(slot, shifted(gx, dx, ngx), shifted(gz, dz, ngz))
                return carry
            lax.fori_loop(0, peers, body, 0)

    def greet(slot, tx, tz):
        pl.semaphore_signal(barrier, inc=1, device_id=(tx, tz), device_id_type=MESH)

    each_peer(greet)
    load.wait()
    best = None
    for row in range(0, rows, 8):
        cons = [xpad[var, pl.ds(halo + row, 8), :] for var in range(5)]
        inverse, vel, pressure = pressure_velocity(cons)
        sound = jnp.sqrt(GAMMA * pressure * inverse)
        local = [jnp.abs(v) + sound for v in vel]
        best = local if best is None else [jnp.maximum(a, b) for a, b in zip(best, local)]
    tops = [jnp.max(jnp.max(b, axis=1, keepdims=True), axis=0, keepdims=True) for b in best]
    lane = lax.broadcasted_iota(jnp.int32, (1, 128), 1)
    mine[...] = jnp.where(lane == 0, tops[0], jnp.where(lane == 1, tops[1], tops[2]))
    for var in range(5):
        zt[var, pl.ds(8, 128), :] = xpad[var, pl.ds(halo, rows), :].T

    pl.semaphore_wait(barrier, peers)

    def send(slot, tx, tz):
        pltpu.make_async_remote_copy(
            src_ref=mine, dst_ref=slots.at[slot], send_sem=send_sem, recv_sem=recv_sem,
            device_id=(tx, tz), device_id_type=MESH,
        ).start()

    each_peer(send)
    right, left = shifted(gx, 1, ngx), shifted(gx, ngx - 1, ngx)
    high, low = shifted(gz, 1, ngz), shifted(gz, ngz - 1, ngz)
    moves = [
        (zt.at[:, pl.ds(8, 8), :], zt.at[:, pl.ds(136, 8), :], (gx, low)),
        (zt.at[:, pl.ds(128, 8), :], zt.at[:, pl.ds(0, 8), :], (gx, high)),
        (xpad.at[:, pl.ds(halo, halo), :], xpad.at[:, pl.ds(halo + rows, halo), :], (left, gz)),
        (xpad.at[:, pl.ds(rows, halo), :], xpad.at[:, pl.ds(0, halo), :], (right, gz)),
    ]
    copies = []
    for index, (src, dst, target) in enumerate(moves):
        copy = pltpu.make_async_remote_copy(
            src_ref=src, dst_ref=dst, send_sem=halo_send.at[index], recv_sem=halo_recv.at[index],
            device_id=target, device_id_type=MESH,
        )
        copy.start()
        copies.append(copy)
    pltpu.make_async_copy(slots, slots, recv_sem).wait()
    alpha_ref[...] = jnp.maximum(jnp.max(slots[...], axis=0), mine[...])
    for copy in copies:
        copy.wait()
    pltpu.make_async_copy(slots, slots, send_sem).wait()


class Line:
    def __init__(self, load):
        self.load = functools.lru_cache(None)(load)
        self.D = functools.lru_cache(None)(lambda j: self.load(j + 1) - self.load(j))
        self.S = functools.lru_cache(None)(lambda j: self.D(j) - self.D(j - 1))
        self.T = functools.lru_cache(None)(lambda j: self.S(j + 1) - self.S(j))
        self.S2 = functools.lru_cache(None)(lambda j: self.S(j) + self.S(j))
        self.C = functools.lru_cache(None)(
            lambda j: (self.S(j) * self.S(j) * (4.0 / 3.0) + 4.0 * EPS_WENO)
            + self.D(j) * self.D(j - 1)
        )

    def L(self, j):
        return self.C(j) + self.S2(j) * self.D(j)

    def R(self, j):
        return self.C(j) - self.S2(j) * self.D(j - 1)


def correction(near, mid, far, t_near, t_far):
    a, b, c = mid * far, near * far, near * mid
    w_near = a * a
    w_far = 3.0 * (c * c)
    total = w_near + 6.0 * (b * b) + w_far
    return (w_far * t_far + (w_near + w_near) * t_near) * reciprocal(total)


def line_divergence(count, load_plus, load_minus, emit):
    plus, minus = Line(load_plus), Line(load_minus)
    twice = functools.lru_cache(None)(lambda j: plus.load(j) + minus.load(j))

    def face(j):
        up = correction(plus.L(j - 1), plus.C(j), plus.R(j + 1), plus.T(j - 1), plus.T(j))
        down = correction(minus.R(j + 2), minus.C(j + 1), minus.L(j), minus.T(j + 1), minus.T(j))
        return (
            3.0 * (twice(j) + twice(j + 1)) - (plus.S(j) + minus.S(j + 1)) - up + down
        )

    before = face(2)
    for cell in range(count):
        j = cell + 3
        after = face(j)
        central = (
            4.5 * (twice(j + 1) - twice(j - 1))
            - 0.9 * (twice(j + 2) - twice(j - 2))
            + 0.1 * (twice(j + 3) - twice(j - 3))
        )
        emit(cell, after - before, central)
        before = after


def split_fluxes(cons, var, alpha, fp, fm, cell):
    _, vel, pressure = pressure_velocity(cons)
    velocity = vel[var - 1]
    for field in range(5):
        if field == 4:
            flux = (cons[4] + pressure) * velocity
        else:
            flux = cons[field] * velocity
        if field == var:
            flux = flux + pressure
        drift = alpha * cons[field]
        fp[field, cell] = flux + drift
        fm[field, cell] = flux - drift


def update_kernel(
    cx, ny, xpad, zt, alpha_ref, register, top_ghost, flags, new_state, new_register,
    mask, mask_t, acc, acc_t, fp, fm
):
    halo = 3 * ny
    rows = cx * ny
    strip = zt.shape[1] - 16
    chunk = strip // 8
    alpha = [jnp.broadcast_to(alpha_ref[:, k : k + 1], (8, 128)) for k in range(3)]
    mask[...] = jnp.broadcast_to(flags[...], (rows, 128)).astype(jnp.float32)
    mask_t[...] = mask[...].T[:8]

    for cell in range(chunk + 6):
        cons = [zt[f, pl.ds(5 + cell, 8, stride=chunk), :] for f in range(5)]
        split_fluxes(cons, 3, alpha[2], fp, fm, cell)
    flag_t = mask_t[...] > 0.0

    def z_field(f, carry):
        def emit(cell, upwind, central):
            acc_t[f, pl.ds(cell, 8, stride=chunk), :] = (LAMBDA[2] / 12.0) * jnp.where(
                flag_t, upwind, central
            )
        line_divergence(chunk, lambda j: fp[f, j], lambda j: fm[f, j], emit)
        return carry

    lax.fori_loop(0, 5, z_field, 0)

    for part in range(0, ny, 8):
        for cell in range(cx + 6):
            cons = [xpad[f, pl.ds(cell * ny + part, 8), :] for f in range(5)]
            split_fluxes(cons, 1, alpha[0], fp, fm, cell)

        def x_field(f, carry):
            def emit(cell, upwind, central):
                where = pl.ds(cell * ny + part, 8)
                acc[f, where, :] = (LAMBDA[0] / 12.0) * jnp.where(
                    mask[where, :] > 0.0, upwind, central
                )
            line_divergence(cx, lambda j: fp[f, j], lambda j: fm[f, j], emit)
            return carry

        lax.fori_loop(0, 5, x_field, 0)

    for cell in range(ny + 6):
        y = cell - 3
        if y < ny:
            source = y if y >= 0 else -1 - y
            cons = [xpad[f, pl.ds(halo + source, 8, stride=ny), :] for f in range(5)]
            if y < 0:
                cons[2] = -cons[2]
        else:
            cons = [top_ghost[f, :, y - ny, :] for f in range(5)]
        split_fluxes(cons, 2, alpha[1], fp, fm, cell)

    def y_field(f, carry):
        def emit(cell, upwind, central):
            where = pl.ds(cell, 8, stride=ny)
            acc[f, where, :] = acc[f, where, :] + (LAMBDA[1] / 12.0) * jnp.where(
                mask[where, :] > 0.0, upwind, central
            )
        line_divergence(ny, lambda j: fp[f, j], lambda j: fm[f, j], emit)
        return carry

    lax.fori_loop(0, 5, y_field, 0)

    for f in range(5):
        total = acc[f] + acc_t[f].T
        updated = REGISTER_DECAY * register[f] - total
        new_register[f] = updated
        new_state[f] = xpad[f, pl.ds(halo, rows), :] + UPDATE_WEIGHT * updated


def shards(ngx, ngz, state, register, top_ghost, flags):
    _, cx, ny, cz = state.shape
    rows = cx * ny
    vmem = pl.BlockSpec(memory_space=pltpu.VMEM)
    flat = state.reshape(5, rows, cz)
    peers = ngx * ngz - 1
    f32 = jnp.float32
    xpad, zt, alpha = pl.pallas_call(
        functools.partial(exchange_kernel, ngx, ngz, ny),
        out_shape=(
            jax.ShapeDtypeStruct((5, (cx + 6) * ny, cz), f32),
            jax.ShapeDtypeStruct((5, cz + 16, rows), f32),
            jax.ShapeDtypeStruct((1, 128), f32),
        ),
        in_specs=[pl.BlockSpec(memory_space=pl.ANY)],
        out_specs=[vmem] * 3,
        scratch_shapes=[
            pltpu.VMEM((peers, 1, 128), f32),
            pltpu.VMEM((1, 128), f32),
            pltpu.SemaphoreType.DMA,
            pltpu.SemaphoreType.DMA,
            pltpu.SemaphoreType.DMA,
            pltpu.SemaphoreType.DMA((4,)),
            pltpu.SemaphoreType.DMA((4,)),
        ],
        compiler_params=pltpu.CompilerParams(collective_id=0, has_side_effects=True),
        name="exchange",
    )(flat)
    longest = max(cx, ny, cz // 8) + 6
    new_state, new_register = pl.pallas_call(
        functools.partial(update_kernel, cx, ny),
        out_shape=(jax.ShapeDtypeStruct((5, rows, cz), f32),) * 2,
        in_specs=[vmem] * 6,
        out_specs=[vmem] * 2,
        scratch_shapes=[
            pltpu.VMEM((rows, 128), f32),
            pltpu.VMEM((8, 128), f32),
            pltpu.VMEM((5, rows, cz), f32),
            pltpu.VMEM((5, cz, rows), f32),
            pltpu.VMEM((5, longest, 8, 128), f32),
            pltpu.VMEM((5, longest, 8, 128), f32),
        ],
        name="update",
    )(xpad, zt, alpha, register.reshape(5, rows, cz), top_ghost, flags.reshape(rows, 1))
    return new_state.reshape(state.shape), new_register.reshape(state.shape)


def solution(mesh):
    block = P(None, "gx", None, "gz")
    return jax.shard_map(
        functools.partial(shards, mesh.shape["gx"], mesh.shape["gz"]),
        mesh=mesh,
        in_specs=(block, block, block, P("gx", None, "gz")),
        out_specs=(block, block),
        check_vma=False,
    )
```

time: 67.2 us -> 23.9 us (0.36)
  blocking collectives: 37.7 us -> 0 us
  Pallas kernels: 0 us -> 20.3 us
  other arithmetic: 16.2 us -> 0.66 us
  starting transfers between devices: 7.66 us -> 0 us
  local copies, waits for them, and re-layouts: 4.38 us -> 2.04 us
    pmax x1 -> x0, blocking collectives: 37.7 us -> none  [global_speeds(): return lax.pmax(local, ('gx', 'gz'))]
    pallas_call x0 -> x2, Pallas kernels: none -> 20.3 us  [the longest x1 14 us: shards(): pl.pallas_call(functools.partial(exchange_kernel, ngx, ngz, ny), out_shap...]
    ppermute x4 -> x0, starting transfers between devices: 7.66 us -> none  [the longest x2 4.57 us: extended(): lax.ppermute(lax.slice_in_dim(block, 0, width, axis=dim), axis, backward)]
    add x3 -> x0, other arithmetic: 7.21 us -> none  [the longest x2 6.6 us: divergence(): upwind + weno_face([window(minus, 5), window(minus, 4), window(minus, 3),...]
    div x3 -> x0, other arithmetic: 2.93 us -> none  [divergence(): (37.0 * (window(flux, 2) + window(flux, 3)) - 8.0 * (window(flux, 1) + wi...]
    mul x4 -> x0, other arithmetic: 2.47 us -> none  [the longest x3 2.39 us: divergence(): plus = 0.5 * (flux + alpha * padded)]
    unnamed x13 -> x6, local copies, waits for them, and re-layouts: 3.47 us -> 1.33 us
    another operation x4 -> x0, other arithmetic: 2.08 us -> none  [the longest x1 2 us: global_speeds(): jnp.stack([jnp.max(jnp.abs(vel_x) + sound), jnp.max(jnp.abs(vel_y) + soun...]
  transfers between devices with their start and end apart: 4 -> 0, of which waited for: 0 -> 0; matrix products, arithmetic and copies ran while one was open for 17% -> 0% of each run, Pallas kernels for 0% -> 0%
where the time goes in v1:
time: 23.9 us; the launch traced here: 23.7 us
  Pallas kernels  20.3 us (85%)
  local copies, waits for them, and re-layouts  2.04 us (9%)
  other arithmetic  0.66 us (3%)
  between operations  0.66 us (3%)
    pallas_call x1, Pallas kernels, shards(): pl.pallas_call(functools.partial(exchange_kernel, ngx, ngz, ny), out_shap...  14 us
    pallas_call x1, Pallas kernels, shards(): pl.pallas_call(functools.partial(update_kernel, cx, ny), out_shape=(jax.S...  6.29 us
    unnamed x6, local copies, waits for them, and re-layouts  1.33 us
    reshape x1, local copies, waits for them, and re-layouts, shards(): flags.reshape(rows, 1)  0.72 us
    unnamed x1, other arithmetic  0.66 us

profile of v1, /device:TPU:0, one launch (start us, length us, event | category | flops | bytes accessed | tf_op | source)
XLA Modules:
  0.0 23.7 jit_solution(6705014027259622979)
XLA Ops:
  0.6 0.0 copy-start.1
  0.6 0.0 copy-start
  0.6 0.5 %broadcast.3 = s32[]{:T(128)} broadcast(s32[]{:T(128)} %constant.7), dimensions={} | broadcast | bytes 8 | tf_op args[3]
  1.2 0.2 copy-done.1
  1.3 0.7 %reduce.3 = s32[8,16]{1,0:T(8,128)S(1)} reduce(s32[8,16,1]{1,2,0:T(1,128)S(1)} %copy-done.1, s32[]{:T(128)} %broadcast.3), dimensions={2}, to_apply=%param.7.reduce_sub_computation.3 | reduce | bytes 1028 | tf_op args[3]
  2.0 0.7 %reshape.24.flags = s32[128,1]{1,0:T(8,128)} reshape(s32[8,16]{1,0:T(8,128)S(1)} %reduce.3) | data formatting | bytes 1024 | tf_op jit(solution)/shard_map/reshape | solution.py:293
  2.7 0.0 copy-done
  2.7 0.7 %copy.6.top_ghost = f32[5,8,3,128]{3,2,1,0:T(4,128)} copy(f32[5,8,3,128]{3,1,2,0:T(8,128)S(1)} %copy-done) | data formatting | bytes 122880 | tf_op args[2]
  3.4 14.0 %exchange.1 = (f32[5,224,128]{2,1,0:T(8,128)}, f32[5,144,128]{2,1,0:T(8,128)}, f32[1,128]{1,0:T(1,128)}) custom-call(f32[5,128,128]{2,1,0:T(8,128)} %bitcast.6), custom_call_target="tpu_custom_call" | custom-call | tf_op jit(solution)/shard_map/exchange/pallas_call | solution.py:257
  17.4 6.3 %update.1 = (f32[5,128,128]{2,1,0:T(8,128)}, f32[5,128,128]{2,1,0:T(8,128)}) custom-call(f32[5,224,128]{2,1,0:T(8,128)} %get-tuple-element.7.xpad, f32[5,144,128]{2,1,0:T(8,128)} %get-tuple-element.8.zt, f32[1,128]{1,0:T(1,128)} %get-tuple-element.9.alpha_ref, f32[5,128,128]{2,1,0:T(8,128)} %bitcast.5, f32[5,8,3,128]{3,2,1,0:T(4,128)} %copy.6.top_ghost, ...), custom_call_target="tpu_custom_call" | custom-call | tf_op jit(solution)/shard_map/update/pallas_call | solution.py:279
Async XLA Ops:
  0.6 0.7 %copy-start.1 = (s32[8,16,1]{1,2,0:T(1,128)S(1)}, s32[8,16,1]{1,2,0:T(1,128)}, u32[]{:S(2)}) copy-start(s32[8,16,1]{1,2,0:T(1,128)} %param.7) | copy-start | bytes 1540
  0.6 2.1 %copy-start = (f32[5,8,3,128]{3,1,2,0:T(8,128)S(1)}, f32[5,8,3,128]{3,1,2,0:T(8,128)}, u32[]{:S(2)}) copy-start(f32[5,8,3,128]{3,1,2,0:T(8,128)} %param.6) | copy-start | bytes 184324

commit v2 on v1

v2 whole, which is shorter than its diff:
```python
import functools

import jax
import jax.numpy as jnp
from jax import lax
from jax.experimental import pallas as pl
from jax.experimental.pallas import tpu as pltpu
from jax.sharding import PartitionSpec as P

MESH = pl.DeviceIdType.MESH
GAMMA = 1.4
EPS_WENO = 1e-06
LAMBDA = (0.1, 0.15, 0.1)
REGISTER_DECAY = -5.0 / 9.0
UPDATE_WEIGHT = 15.0 / 16.0
UNROLL_LIMIT = 64


def reciprocal(value):
    guess = pl.reciprocal(value, approx=True)
    return guess * (2.0 - value * guess)


def pressure_velocity(cons):
    inverse = reciprocal(cons[0])
    vel = [cons[1] * inverse, cons[2] * inverse, cons[3] * inverse]
    pressure = (GAMMA - 1.0) * (
        cons[4] - 0.5 * (cons[1] * vel[0] + cons[2] * vel[1] + cons[3] * vel[2])
    )
    return inverse, vel, pressure


def shifted(me, step, count):
    moved = me + step
    return jnp.where(moved >= count, moved - count, moved)


def exchange_peers(gx, gz, ngx, ngz):
    offsets = [(dx, dz) for dx in range(ngx) for dz in range(ngz)][1:]

    def each_peer(action):
        if len(offsets) < UNROLL_LIMIT:
            for slot, (dx, dz) in enumerate(offsets):
                action(slot, shifted(gx, dx, ngx), shifted(gz, dz, ngz))
        else:
            def body(slot, carry):
                dx, dz = (slot + 1) // ngz, (slot + 1) % ngz
                action(slot, shifted(gx, dx, ngx), shifted(gz, dz, ngz))
                return carry
            lax.fori_loop(0, len(offsets), body, 0)

    return each_peer, len(offsets)


class Line:
    def __init__(self, load):
        cached = functools.lru_cache(None)
        self.load = cached(load)
        self.D = cached(lambda j: self.load(j + 1) - self.load(j))
        self.S = cached(lambda j: self.D(j) - self.D(j - 1))
        self.T = cached(lambda j: self.S(j + 1) - self.S(j))
        self.S2 = cached(lambda j: self.S(j) + self.S(j))
        self.C = cached(
            lambda j: (self.S(j) * self.S(j) * (4.0 / 3.0) + 4.0 * EPS_WENO)
            + self.D(j) * self.D(j - 1)
        )

    def L(self, j):
        return self.C(j) + self.S2(j) * self.D(j)

    def R(self, j):
        return self.C(j) - self.S2(j) * self.D(j - 1)


def correction(near, mid, far, t_near, t_far):
    a, b, c = mid * far, near * far, near * mid
    w_near = a * a
    w_far = 3.0 * (c * c)
    total = w_near + 6.0 * (b * b) + w_far
    return (w_far * t_far + (w_near + w_near) * t_near) * reciprocal(total)


def line_divergence(count, alpha, load_flux, load_cons, emit):
    flux = functools.lru_cache(None)(load_flux)
    drift = functools.lru_cache(None)(lambda j: alpha * load_cons(j))
    plus, minus = Line(lambda j: flux(j) + drift(j)), Line(lambda j: flux(j) - drift(j))

    def face(j):
        up = correction(plus.L(j - 1), plus.C(j), plus.R(j + 1), plus.T(j - 1), plus.T(j))
        down = correction(minus.R(j + 2), minus.C(j + 1), minus.L(j), minus.T(j + 1), minus.T(j))
        return 6.0 * (flux(j) + flux(j + 1)) - (plus.S(j) + minus.S(j + 1)) - up + down

    before = face(2)
    for cell in range(count):
        j = cell + 3
        after = face(j)
        central = (
            9.0 * (flux(j + 1) - flux(j - 1))
            - 1.8 * (flux(j + 2) - flux(j - 2))
            + 0.2 * (flux(j + 3) - flux(j - 3))
        )
        emit(cell, after - before, central)
        before = after


def store_fluxes(cons, var, fluxes, conserved, cell):
    _, vel, pressure = pressure_velocity(cons)
    velocity = vel[var - 1]
    for field in range(5):
        if field == 4:
            flux = (cons[4] + pressure) * velocity
        else:
            flux = cons[field] * velocity
        if field == var:
            flux = flux + pressure
        fluxes[field, cell] = flux
        conserved[field, cell] = cons[field]


def step_kernel(
    ngx, ngz, cx, ny, state_ref, ghost_ref, flags_ref, change_ref, xpad, zt, ghost, flags,
    slots, mine, mask, acc, acc_t, zf, zu, yf, yu, xf, xu,
    load_sem, side_sem, send_sem, recv_sem, halo_send, halo_recv, out_sem
):
    gx, gz = lax.axis_index("gx"), lax.axis_index("gz")
    rows = cx * ny
    halo = 3 * ny
    strip = zt.shape[1] - 16
    chunk = strip // 8
    load = pltpu.make_async_copy(state_ref, xpad.at[:, pl.ds(halo, rows), :], load_sem)
    load.start()
    load_flags = pltpu.make_async_copy(flags_ref, flags, side_sem.at[0])
    load_flags.start()
    load_ghost = pltpu.make_async_copy(ghost_ref, ghost, side_sem.at[1])
    load_ghost.start()
    barrier = pltpu.get_barrier_semaphore()
    each_peer, peers = exchange_peers(gx, gz, ngx, ngz)

    def greet(slot, tx, tz):
        pl.semaphore_signal(barrier, inc=1, device_id=(tx, tz), device_id_type=MESH)

    each_peer(greet)
    load.wait()
    best = None
    for row in range(0, rows, 8):
        cons = [xpad[var, pl.ds(halo + row, 8), :] for var in range(5)]
        inverse, vel, pressure = pressure_velocity(cons)
        sound = jnp.sqrt(GAMMA * pressure * inverse)
        local = [jnp.abs(v) + sound for v in vel]
        best = local if best is None else [jnp.maximum(a, b) for a, b in zip(best, local)]
    tops = [jnp.max(jnp.max(b, axis=0, keepdims=True), axis=1, keepdims=True) for b in best]
    lane = lax.broadcasted_iota(jnp.int32, (1, 128), 1)
    mine[...] = jnp.where(lane == 0, tops[0], jnp.where(lane == 1, tops[1], tops[2]))

    pl.semaphore_wait(barrier, peers)

    def send(slot, tx, tz):
        pltpu.make_async_remote_copy(
            src_ref=mine, dst_ref=slots.at[slot], send_sem=send_sem, recv_sem=recv_sem,
            device_id=(tx, tz), device_id_type=MESH,
        ).start()

    each_peer(send)
    right, left = shifted(gx, 1, ngx), shifted(gx, ngx - 1, ngx)
    high, low = shifted(gz, 1, ngz), shifted(gz, ngz - 1, ngz)

    def move(index, src, dst, target):
        copy = pltpu.make_async_remote_copy(
            src_ref=src, dst_ref=dst, send_sem=halo_send.at[index], recv_sem=halo_recv.at[index],
            device_id=target, device_id_type=MESH,
        )
        copy.start()
        return copy

    x_copies = [
        move(0, xpad.at[:, pl.ds(halo, halo), :], xpad.at[:, pl.ds(halo + rows, halo), :], (left, gz)),
        move(1, xpad.at[:, pl.ds(rows, halo), :], xpad.at[:, pl.ds(0, halo), :], (right, gz)),
    ]
    for var in range(5):
        zt[var, pl.ds(8, strip), :] = xpad[var, pl.ds(halo, rows), :].T
    load_flags.wait()
    for x in range(cx):
        wide = jnp.broadcast_to(flags[x], (strip, ny)).astype(jnp.float32)
        mask[pl.ds(x * ny, ny), :] = wide.T
    z_copies = [
        move(2, zt.at[:, pl.ds(8, 8), :], zt.at[:, pl.ds(8 + strip, 8), :], (gx, low)),
        move(3, zt.at[:, pl.ds(strip, 8), :], zt.at[:, pl.ds(0, 8), :], (gx, high)),
    ]
    flag_t = mask[...].T[:8] > 0.0

    load_ghost.wait()
    for cell in range(ny + 6):
        y = cell - 3
        if y < ny:
            source = y if y >= 0 else -1 - y
            cons = [xpad[f, pl.ds(halo + source, 8, stride=ny), :] for f in range(5)]
            if y < 0:
                cons[2] = -cons[2]
        else:
            cons = [ghost[f, y - ny] for f in range(5)]
        store_fluxes(cons, 2, yf, yu, cell)

    for copy in z_copies:
        copy.wait()
    for cell in range(chunk + 6):
        cons = [zt[f, pl.ds(5 + cell, 8, stride=chunk), :] for f in range(5)]
        store_fluxes(cons, 3, zf, zu, cell)

    pltpu.make_async_copy(slots, slots, recv_sem).wait()
    top = jnp.maximum(jnp.max(slots[...], axis=0), mine[...])
    alpha = [jnp.broadcast_to(top[:, k : k + 1], (8, 128)) for k in range(3)]

    def z_field(f, carry):
        def emit(cell, upwind, central):
            acc_t[f, pl.ds(cell, 8, stride=chunk), :] = (LAMBDA[2] / 12.0) * jnp.where(
                flag_t, upwind, central
            )
        line_divergence(chunk, alpha[2], lambda j: zf[f, j], lambda j: zu[f, j], emit)
        return carry

    lax.fori_loop(0, 5, z_field, 0)
    for f in range(5):
        acc[f] = acc_t[f].T

    def y_field(f, carry):
        def emit(cell, upwind, central):
            where = pl.ds(cell, 8, stride=ny)
            acc[f, where, :] = acc[f, where, :] + (LAMBDA[1] / 12.0) * jnp.where(
                mask[where, :] > 0.0, upwind, central
            )
        line_divergence(ny, alpha[1], lambda j: yf[f, j], lambda j: yu[f, j], emit)
        return carry

    lax.fori_loop(0, 5, y_field, 0)

    for copy in x_copies:
        copy.wait()
    for part in range(ny // 8):
        for cell in range(cx + 6):
            cons = [xpad[f, pl.ds(cell * ny + part * 8, 8), :] for f in range(5)]
            store_fluxes(cons, 1, xf.at[part], xu.at[part], cell)

    def x_field(f, carry):
        for part in range(ny // 8):
            def emit(cell, upwind, central):
                where = pl.ds(cell * ny + part * 8, 8)
                acc[f, where, :] = acc[f, where, :] + (LAMBDA[0] / 12.0) * jnp.where(
                    mask[where, :] > 0.0, upwind, central
                )
            line_divergence(
                cx, alpha[0], lambda j: xf[part, f, j], lambda j: xu[part, f, j], emit
            )
        pltpu.make_async_copy(acc.at[f], change_ref.at[f], out_sem).start()
        return carry

    lax.fori_loop(0, 5, x_field, 0)
    pltpu.make_async_copy(slots, slots, send_sem).wait()
    pltpu.make_async_copy(acc, change_ref, out_sem).wait()


def shards(ngx, ngz, state, register, top_ghost, flags):
    _, cx, ny, cz = state.shape
    rows = cx * ny
    peers = ngx * ngz - 1
    f32 = jnp.float32
    anywhere = pl.BlockSpec(memory_space=pl.ANY)
    flat = state.reshape(5, rows, cz)
    change = pl.pallas_call(
        functools.partial(step_kernel, ngx, ngz, cx, ny),
        out_shape=jax.ShapeDtypeStruct((5, rows, cz), f32),
        in_specs=[anywhere] * 3,
        out_specs=anywhere,
        scratch_shapes=[
            pltpu.VMEM((5, (cx + 6) * ny, cz), f32),
            pltpu.VMEM((5, cz + 16, rows), f32),
            pltpu.VMEM((5, 3, cx, cz), f32),
            pltpu.VMEM((cx, 1, ny), jnp.int32),
            pltpu.VMEM((peers, 1, 128), f32),
            pltpu.VMEM((1, 128), f32),
            pltpu.VMEM((rows, cz), f32),
            pltpu.VMEM((5, rows, cz), f32),
            pltpu.VMEM((5, cz, rows), f32),
            pltpu.VMEM((5, cz // 8 + 6, 8, rows), f32),
            pltpu.VMEM((5, cz // 8 + 6, 8, rows), f32),
            pltpu.VMEM((5, ny + 6, 8, cz), f32),
            pltpu.VMEM((5, ny + 6, 8, cz), f32),
            pltpu.VMEM((ny // 8, 5, cx + 6, 8, cz), f32),
            pltpu.VMEM((ny // 8, 5, cx + 6, 8, cz), f32),
            pltpu.SemaphoreType.DMA,
            pltpu.SemaphoreType.DMA((2,)),
            pltpu.SemaphoreType.DMA,
            pltpu.SemaphoreType.DMA,
            pltpu.SemaphoreType.DMA((4,)),
            pltpu.SemaphoreType.DMA((4,)),
            pltpu.SemaphoreType.DMA,
        ],
        compiler_params=pltpu.CompilerParams(collective_id=0, has_side_effects=True),
        name="step",
    )(flat, top_ghost.transpose(0, 2, 1, 3), flags.transpose(0, 2, 1))
    new_register = REGISTER_DECAY * register - change.reshape(state.shape)
    new_state = state + UPDATE_WEIGHT * new_register
    return new_state, new_register


def solution(mesh):
    block = P(None, "gx", None, "gz")
    return jax.shard_map(
        functools.partial(shards, mesh.shape["gx"], mesh.shape["gz"]),
        mesh=mesh,
        in_specs=(block, block, block, P("gx", None, "gz")),
        out_specs=(block, block),
        check_vma=False,
    )
```

time: 23.9 us -> 17.7 us (0.74)
  Pallas kernels: 20.3 us -> 15 us
  local copies, waits for them, and re-layouts: 2.04 us -> 0.01 us
  other arithmetic: 0.66 us -> 1.88 us
    pallas_call x2 -> x1, Pallas kernels: 20.3 us -> 15 us  [shards(): pl.pallas_call(functools.partial(step_kernel, ngx, ngz, cx, ny), out_shap...]
    add x0 -> x1, other arithmetic: none -> 1.88 us  [shards(): new_state = state + UPDATE_WEIGHT * new_register]
    unnamed x6 -> x4, local copies, waits for them, and re-layouts: 1.33 us -> 0.01 us
    reshape x1 -> x0, local copies, waits for them, and re-layouts: 0.72 us -> none  [shards(): flags.reshape(rows, 1)]
    unnamed x1 -> x0, other arithmetic: 0.66 us -> none
where the time goes in v2:
time: 17.7 us; the launch traced here: 17.5 us
  Pallas kernels  15 us (85%)
  other arithmetic  1.88 us (11%)
  between operations  0.67 us (4%)
    pallas_call x1, Pallas kernels, shards(): pl.pallas_call(functools.partial(step_kernel, ngx, ngz, cx, ny), out_shap...  15 us
    add x1, other arithmetic, shards(): new_state = state + UPDATE_WEIGHT * new_register  1.88 us

profile of v2, /device:TPU:0, one launch (start us, length us, event | category | flops | bytes accessed | tf_op | source)
XLA Modules:
  0.0 17.5 jit_solution(5797052314003363186)
XLA Ops:
  0.6 0.0 copy-start
  0.6 0.0 copy-start.1
  0.7 15.0 %step.1 = f32[5,128,128]{2,1,0:T(8,128)} custom-call(f32[5,128,128]{2,1,0:T(8,128)} %bitcast.6, f32[5,3,8,128]{3,2,1,0:T(8,128)} %bitcast.8, s32[8,1,16]{2,1,0:T(1,128)} %bitcast.9), custom_call_target="tpu_custom_call" | custom-call | tf_op jit(solution)/shard_map/step/pallas_call | solution.py:268
  15.6 0.0 copy-done
  15.6 0.0 copy-done.1
  15.7 1.9 %multiply_add_fusion = (f32[5,8,16,128]{3,2,1,0:T(8,128)}, f32[5,8,16,128]{3,2,1,0:T(8,128)}) fusion(f32[5,8,16,128]{3,2,1,0:T(8,128)S(1)} %copy-done, f32[5,8,16,128]{3,2,1,0:T(8,128)} %bitcast.7, f32[5,8,16,128]{3,2,1,0:T(8,128)S(1)} %copy-done.1), kind=kLoop, calls=%fused_computation | loop fusion | flops 327680 | bytes 1638400 | tf_op jit(solution)/shard_map/add | solution.py:301
Async XLA Ops:
  0.6 15.0 %copy-start = (f32[5,8,16,128]{3,2,1,0:T(8,128)S(1)}, f32[5,8,16,128]{3,2,1,0:T(8,128)}, u32[]{:S(2)}) copy-start(f32[5,8,16,128]{3,2,1,0:T(8,128)} %param.4) | copy-start | bytes 983044
  0.6 15.0 %copy-start.1 = (f32[5,8,16,128]{3,2,1,0:T(8,128)S(1)}, f32[5,8,16,128]{3,2,1,0:T(8,128)}, u32[]{:S(2)}) copy-start(f32[5,8,16,128]{3,2,1,0:T(8,128)} %param.5) | copy-start | bytes 983044

commit v3 on v2

--- a/solution.py
+++ b/solution.py
@@ -118,8 +118,8 @@
 
 
 def step_kernel(
-    ngx, ngz, cx, ny, state_ref, ghost_ref, flags_ref, change_ref, xpad, zt, ghost, flags,
-    slots, mine, mask, acc, acc_t, zf, zu, yf, yu, xf, xu,
+    ngx, ngz, cx, ny, state_ref, ghost_ref, flags_ref, acc, xpad, zt, ghost, flags,
+    slots, mine, mask, acc_t, zf, zu, yf, yu, xf, xu,
     load_sem, side_sem, send_sem, recv_sem, halo_send, halo_recv, out_sem
 ):
     gx, gz = lax.axis_index("gx"), lax.axis_index("gz")
@@ -250,12 +250,10 @@
             line_divergence(
                 cx, alpha[0], lambda j: xf[part, f, j], lambda j: xu[part, f, j], emit
             )
-        pltpu.make_async_copy(acc.at[f], change_ref.at[f], out_sem).start()
         return carry
 
     lax.fori_loop(0, 5, x_field, 0)
     pltpu.make_async_copy(slots, slots, send_sem).wait()
-    pltpu.make_async_copy(acc, change_ref, out_sem).wait()
 
 
 def shards(ngx, ngz, state, register, top_ghost, flags):
@@ -267,9 +265,9 @@
     flat = state.reshape(5, rows, cz)
     change = pl.pallas_call(
         functools.partial(step_kernel, ngx, ngz, cx, ny),
-        out_shape=jax.ShapeDtypeStruct((5, rows, cz), f32),
+        out_shape=pltpu.VMEM((5, rows, cz), f32),
         in_specs=[anywhere] * 3,
-        out_specs=anywhere,
+        out_specs=pl.BlockSpec(memory_space=pltpu.VMEM),
         scratch_shapes=[
             pltpu.VMEM((5, (cx + 6) * ny, cz), f32),
             pltpu.VMEM((5, cz + 16, rows), f32),
@@ -278,7 +276,6 @@
             pltpu.VMEM((peers, 1, 128), f32),
             pltpu.VMEM((1, 128), f32),
             pltpu.VMEM((rows, cz), f32),
-            pltpu.VMEM((5, rows, cz), f32),
             pltpu.VMEM((5, cz, rows), f32),
             pltpu.VMEM((5, cz // 8 + 6, 8, rows), f32),
             pltpu.VMEM((5, cz // 8 + 6, 8, rows), f32),

time: 17.7 us -> 16.1 us (0.910)
  other arithmetic: 1.88 us -> 0.92 us
  Pallas kernels: 15 us -> 14.3 us
    add x1, other arithmetic: 1.88 us -> 0.92 us  [shards(): new_state = state + UPDATE_WEIGHT * new_register]
    pallas_call x1, Pallas kernels: 15 us -> 14.3 us  [shards(): pl.pallas_call(functools.partial(step_kernel, ngx, ngz, cx, ny), out_shap...]
where the time goes in v3:
time: 16.1 us; the launch traced here: 16 us
  Pallas kernels  14.3 us (89%)
  other arithmetic  0.92 us (6%)
  between operations  0.67 us (4%)
    pallas_call x1, Pallas kernels, shards(): pl.pallas_call(functools.partial(step_kernel, ngx, ngz, cx, ny), out_shap...  14.3 us
    add x1, other arithmetic, shards(): new_state = state + UPDATE_WEIGHT * new_register  0.92 us

profile of v3, /device:TPU:0, one launch (start us, length us, event | category | flops | bytes accessed | tf_op | source)
XLA Modules:
  0.0 16.0 jit_solution(11628981123872618397)
XLA Ops:
  0.6 0.0 copy-start
  0.6 0.0 copy-start.1
  0.7 14.3 %step.1 = f32[5,128,128]{2,1,0:T(8,128)S(1)} custom-call(f32[5,128,128]{2,1,0:T(8,128)} %bitcast.7, f32[5,3,8,128]{3,2,1,0:T(8,128)} %bitcast.8, s32[8,1,16]{2,1,0:T(1,128)} %bitcast.9), custom_call_target="tpu_custom_call" | custom-call | tf_op jit(solution)/shard_map/step/pallas_call | solution.py:266
  15.0 0.0 copy-done
  15.0 0.0 copy-done.1
  15.0 0.9 %multiply_add_fusion = (f32[5,8,16,128]{3,2,1,0:T(8,128)}, f32[5,8,16,128]{3,2,1,0:T(8,128)}) fusion(f32[5,8,16,128]{3,2,1,0:T(8,128)S(1)} %copy-done, f32[5,8,16,128]{3,2,1,0:T(8,128)S(1)} %bitcast.6, f32[5,8,16,128]{3,2,1,0:T(8,128)S(1)} %copy-done.1), kind=kLoop, calls=%fused_computation | loop fusion | flops 327680 | bytes 1638400 | tf_op jit(solution)/shard_map/add | solution.py:298
Async XLA Ops:
  0.6 14.4 %copy-start = (f32[5,8,16,128]{3,2,1,0:T(8,128)S(1)}, f32[5,8,16,128]{3,2,1,0:T(8,128)}, u32[]{:S(2)}) copy-start(f32[5,8,16,128]{3,2,1,0:T(8,128)} %param.4) | copy-start | bytes 983044
  0.6 14.4 %copy-start.1 = (f32[5,8,16,128]{3,2,1,0:T(8,128)S(1)}, f32[5,8,16,128]{3,2,1,0:T(8,128)}, u32[]{:S(2)}) copy-start(f32[5,8,16,128]{3,2,1,0:T(8,128)} %param.5) | copy-start | bytes 983044
